TPU v7x, 32 devices: a whole 2x2x4 slice. The times are simulated.
32 devices in a mesh: gx: 4 (over y, core), gy: 8 (over z, x).
Axes of the slice: x: 2, y: 2, z: 4, core: 2. Of those that a mesh axis runs over, the one named last changes fastest.
Arguments:
- previous: float32 [2, 7, 512, 1024], P(None, None, 'gx', 'gy'), may hold values from -6 to 6
- dissipated: float32 [2, 4, 512, 1024], P(None, None, 'gx', 'gy'), may hold values from 0.05 to 3
- material: int32 [4, 512, 1024], P(None, 'gx', 'gy'), may hold values from 0 to 3
- coolant: int32 [3, 512, 1024], P(None, 'gx', 'gy'), may hold values from 0 to 3
Outputs:
- temperature: float32 [2, 7, 512, 1024], P(None, None, 'gx', 'gy')
All inputs are finite; a program needn't handle non-finite values.
Results may differ from a plain program's by a relative error of at most 0.00011.
Values sent between devices are 32-bit elements; how exact they have to be, the bound alone decides.
A program may use at most 64 MiB of HBM per device.

v0:
```python
import jax
import jax.numpy as jnp
from jax import lax
from jax.sharding import PartitionSpec as P

ITERS = 3
TIER_K = (1.0, 0.3, 0.12, 2.5)
CHANNEL_K = (1.0, 0.3, 0.25, 0.2)
CHANNEL_SINK = (0.0, 0.15, 0.45, 1.2)
TIER_HEAT = 0.05
CHANNEL_HEAT = 0.2
VERTICAL = 4.0


def extended_2(x, sides, width):
    for axis, dim in sides:
        devices, length = (lax.axis_size(axis), x.shape[dim])
        up = [(i, (i + 1) % devices) for i in range(devices - 1)]
        down = [(j, i) for i, j in up]
        last = lax.slice_in_dim(x, length - width, length, axis=dim)
        leading = lax.slice_in_dim(x, 0, width, axis=dim)
        before = lax.ppermute(last, axis, up)
        after = lax.ppermute(leading, axis, down)
        x = jnp.concatenate([before, x, after], axis=dim)
    return x


def lookup(codes, table):
    total = jnp.zeros(codes.shape, jnp.float32)
    for index, value in enumerate(table):
        total = total + jnp.where(codes == index, jnp.float32(value), jnp.float32(0.0))
    return total


def mix(tiers, channels):
    rows = []
    for layer in range(2 * tiers.shape[0] - 1):
        rows.append(tiers[layer // 2] if layer % 2 == 0 else channels[layer // 2])
    return jnp.stack(rows)


def spread_power(heat):
    tiers = heat.shape[1]
    empty = jnp.zeros_like(heat[:, 0])
    rows = []
    for layer in range(2 * tiers - 1):
        rows.append(heat[:, layer // 2] if layer % 2 == 0 else empty)
    return jnp.stack(rows, 1)


def capacity_column(layers):
    return jnp.array(
        [TIER_HEAT if layer % 2 == 0 else CHANNEL_HEAT for layer in range(layers)], jnp.float32
    )


def couplings(padded_k):
    centre = padded_k[:, 1:-1, 1:-1]
    g_north = jnp.sqrt(centre * padded_k[:, :-2, 1:-1])
    g_south = jnp.sqrt(centre * padded_k[:, 2:, 1:-1])
    g_west = jnp.sqrt(centre * padded_k[:, 1:-1, :-2])
    g_east = jnp.sqrt(centre * padded_k[:, 1:-1, 2:])
    g_vertical = VERTICAL * jnp.sqrt(centre[:-1] * centre[1:])
    return (g_north, g_south, g_west, g_east, g_vertical)


def operate(padded_v, padded_k, sink, capacity):
    g_north, g_south, g_west, g_east, g_vertical = couplings(padded_k)
    centre = padded_v[:, :, 1:-1, 1:-1]
    lateral = g_north * (centre - padded_v[:, :, :-2, 1:-1]) + g_south * (
        centre - padded_v[:, :, 2:, 1:-1]
    )
    lateral = (
        lateral
        + g_west * (centre - padded_v[:, :, 1:-1, :-2])
        + g_east * (centre - padded_v[:, :, 1:-1, 2:])
    )
    flux = g_vertical * (centre[:, :-1] - centre[:, 1:])
    zero_row = jnp.zeros_like(centre[:, :1])
    vertical = jnp.concatenate([flux, zero_row], 1) - jnp.concatenate([zero_row, flux], 1)
    return (capacity + sink) * centre + lateral + vertical


def diagonal_terms(padded_k, sink, capacity):
    g_north, g_south, g_west, g_east, g_vertical = couplings(padded_k)
    zero_row = jnp.zeros_like(g_vertical[:1])
    vertical = jnp.concatenate([g_vertical, zero_row], 0) + jnp.concatenate(
        [zero_row, g_vertical], 0
    )
    return capacity + sink + g_north + g_south + g_west + g_east + vertical


def core_sum(first, second):
    return jnp.sum(first * second, axis=(1, 2, 3))


def both_sums(residual, scaled, image):
    return lax.psum((core_sum(residual, scaled), core_sum(scaled, image)), ("gx", "gy"))


def per_device(previous, dissipated, material, coolant):
    tiers = material.shape[0]
    layers = 2 * tiers - 1
    capacity = capacity_column(layers)[:, None, None]
    tier_k = lookup(material, TIER_K)
    kappa = mix(tier_k, lookup(coolant, CHANNEL_K))
    channel_sink = lookup(coolant, CHANNEL_SINK)
    conductivity = extended_2(kappa, (("gx", 1), ("gy", 2)), 1)
    coolant_sink = mix(jnp.zeros_like(tier_k), channel_sink)
    margin_start = 0

    def apply_operator(field, margin):
        extended = extended_2(field, (("gx", 2), ("gy", 3)), 1)
        result = operate(extended, conductivity, coolant_sink, capacity)
        return (result, margin)

    diagonal = diagonal_terms(conductivity, coolant_sink, capacity)
    source = capacity * previous + spread_power(dissipated)
    image, margin = apply_operator(previous, margin_start)
    residual = source - image
    solution = previous
    scaled = residual / diagonal
    image, inner_margin = apply_operator(scaled, margin)
    energy, curvature_now = both_sums(residual, scaled, image)
    step_size = energy / curvature_now
    direction = scaled
    along = image
    margin = inner_margin
    for iteration in range(ITERS):
        solution = solution + step_size[:, None, None, None] * direction
        residual = residual - step_size[:, None, None, None] * along
        if iteration + 1 < ITERS:
            scaled = residual / diagonal
            image, inner_margin = apply_operator(scaled, margin)
            energy_next, curvature_now = both_sums(residual, scaled, image)
            growth = energy_next / energy
            step_size = energy_next / (curvature_now - growth * energy_next / step_size)
            factor = growth[:, None, None, None]
            direction = scaled + factor * direction
            along = image + factor * along
            margin = inner_margin
            energy = energy_next
    return solution


def solution(mesh):
    return jax.shard_map(
        per_device,
        mesh=mesh,
        in_specs=(
            P(None, None, "gx", "gy"),
            P(None, None, "gx", "gy"),
            P(None, "gx", "gy"),
            P(None, "gx", "gy"),
        ),
        out_specs=P(None, None, "gx", "gy"),
        check_vma=False,
    )
```

profile of v0, /device:TPU:0, one launch (start us, length us, event | category | flops | bytes accessed | tf_op | source)
XLA Modules:
  0.0 283.8 jit_solution(1892046935967206937)
XLA Ops:
  1.5 1.3 collective-permute-start.3
  3.3 3.7 %collective-permute-start.1 = (f32[2,7,1,128]{3,1,2,0:T(8,128)}, f32[2,7,1,128]{3,1,2,0:T(8,128)}, u32[]{:S(2)}, u32[]{:S(2)}) collective-permute-start(f32[2,7,1,128]{3,1,2,0:T(8,128)} %copy.160), channel_id=1, source_target_pairs={{0,8},{8,16},{16,24},{1,9},{9,17},{17,25},{2,10},{10,18},{18,26},{... | collective-permute-start | bytes 21512 | tf_op jit(solution)/shard_map/ppermute | solution.py:22
  7.1 1.0 select_add_fusion
  9.0 1.3 collective-permute-start.2
  10.3 4.6 %collective-permute-start = (f32[7,1,128]{2,1,0:T(1,128)}, f32[7,1,128]{2,1,0:T(1,128)S(1)}, u32[]{:S(2)}, u32[]{:S(2)}) collective-permute-start(f32[7,1,128]{2,1,0:T(1,128)} %get-tuple-element.55), channel_id=1, source_target_pairs={{0,8},{8,16},{16,24},{1,9},{9,17},{17,25},{2,10},{10,18},{18,26},{... | collective-permute-start | bytes 10760 | tf_op jit(solution)/shard_map/ppermute | solution.py:22
  21.8 1.1 sqrt_multiply_fusion
  24.7 1.1 fusion.44
  27.0 2.4 stack.15
  30.1 1.1 fusion.80
  31.1 1.3 collective-permute-start.6
  32.4 5.4 %collective-permute-start.4 = (f32[7,130,1]{2,1,0:T(8,128)}, f32[7,130,1]{2,1,0:T(8,128)}, u32[]{:S(2)}, u32[]{:S(2)}) collective-permute-start(f32[7,130,1]{2,1,0:T(8,128)} %get-tuple-element.52), channel_id=1, source_target_pairs={{0,1},{1,2},{2,3},{3,4},{4,5},{5,6},{6,7},{8,9},{9,10},{10,11},{11... | collective-permute-start | bytes 10928 | tf_op jit(solution)/shard_map/ppermute | solution.py:22
  37.8 1.1 copy.121
  40.3 3.6 %collective-permute-start.5 = (f32[2,7,130,1]{2,1,3,0:T(8,128)}, f32[2,7,130,1]{2,1,3,0:T(8,128)S(1)}, u32[]{:S(2)}, u32[]{:S(2)}) collective-permute-start(f32[2,7,130,1]{2,1,3,0:T(8,128)} %get-tuple-element.37), channel_id=1, source_target_pairs={{0,1},{1,2},{2,3},{3,4},{4,5},{5,6},{6,7},{8,9},{9,10},{10,11},{11... | collective-permute-start | bytes 21848 | tf_op jit(solution)/shard_map/ppermute | solution.py:22
  44.0 1.3 collective-permute-start.7
  45.3 1.3 collective-permute-done.6
  46.6 11.4 %collective-permute-done.4 = f32[7,130,1]{2,1,0:T(8,128)} collective-permute-done((f32[7,130,1]{2,1,0:T(8,128)}, f32[7,130,1]{2,1,0:T(8,128)}, u32[]{:S(2)}, u32[]{:S(2)}) %collective-permute-start.4) | collective-permute-done | bytes 3672 | tf_op jit(solution)/shard_map/ppermute | solution.py:22
  58.0 3.0 %add_add_fusion = (f32[7,128,128]{2,1,0:T(8,128)}, f32[7,128,128]{2,1,0:T(8,128)}, f32[7,128,128]{2,1,0:T(8,128)S(1)}, f32[7,128,128]{2,1,0:T(8,128)S(1)}, f32[7...) fusion(f32[6,128,128]{2,1,0:T(8,128)S(1)} %sqrt_multiply_fusion, f32[7,128,128]{2,1,0:T(8,128)S(1)} %copy-done.33, ...), kind=kLoop, calls=%fused_computation.123 | loop fusion | flops 2179072 | bytes 4077708 | tf_op jit(solution)/shard_map/add | solution.py:90
  61.0 2.1 copy.139
  63.1 1.0 copy.119
  65.1 1.0 copy.129
  66.1 1.0 copy.134
  67.2 1.1 copy.117
  68.2 5.3 %broadcast_divide_fusion.2 = (f32[2,7,128,128]{2,1,3,0:T(8,128)S(1)}, f32[2,7,128,128]{2,1,3,0:T(8,128)S(1)}) fusion(f32[7,128,128]{1,0,2:T(8,128)} %copy.139, f32[2,6,128,128]{2,1,3,0:T(8,128)} %fusion.44, f32[2,7,128,128]{2,1,3,0:T(8,128)S(1)} %copy.146, f32[2,7,130,1]{2,1,3,0:T(8,128)} %collective-permute-done.7, f32[2,7,1,128]{2,1,3,0:T(8,128)} %copy-done.26, ...), kind=kLoop, calls=%fused_computation.105 | loop fusion | flops 6193152 | bytes 7237884 | tf_op jit(solution)/shard_map/div | solution.py:122
  73.6 1.3 fusion.77
  75.0 1.6 copy.140
  76.5 2.1 collective-permute-start.8
  79.0 1.3 collective-permute-start.9
  80.3 1.4 copy.141
  82.1 1.4 copy.143
  84.4 4.3 %collective-permute-start.10 = (f32[2,7,130,1]{2,1,3,0:T(8,128)S(1)}, f32[2,7,130,1]{2,1,3,0:T(8,128)S(1)}, u32[]{:S(2)}, u32[]{:S(2)}) collective-permute-start(f32[2,7,130,1]{2,1,3,0:T(8,128)S(1)} %get-tuple-element.35), channel_id=1, source_target_pairs={{0,1},{1,2},{2,3},{3,4},{4,5},{5,6},{6,7},{8,9},{9,10},{10,11},{11... | collective-permute-start | bytes 21848 | tf_op jit(solution)/shard_map/ppermute | solution.py:22
  88.7 1.6 collective-permute-start.11
  90.5 4.2 %collective-permute-done.11 = f32[2,7,130,1]{2,1,3,0:T(8,128)S(1)} collective-permute-done((f32[2,7,130,1]{2,1,3,0:T(8,128)S(1)}, f32[2,7,130,1]{2,1,3,0:T(8,128)S(1)}, u32[]{:S(2)}, u32[]{:S(2)}) %collective-permute-start.11) | collective-permute-done | bytes 7312 | tf_op jit(solution)/shard_map/ppermute | solution.py:23
  94.7 3.0 %multiply_reduce_fusion.3 = (f32[2]{0:T(128)S(1)}, f32[2]{0:T(128)S(1)}, f32[2,7,128,128]{2,1,3,0:T(8,128)}) fusion(f32[2,7,128,128]{2,1,3,0:T(8,128)S(1)} %get-tuple-element.24, f32[2,7,128,128]{2,1,3,0:T(8,128)S(1)} %get-tuple-element.25, f32[2,6,128,128]{2,1,3,0:T(8,128)S(1)} %fusion.30, f32[2,7,130,1]{2,1,3,0:T(8,128)S(1)} %collective-permute-done.11, ...), kind=kLoop, calls=%fused_computation.101 | loop fusion | flops 6193148 | bytes 5861616 | tf_op jit(solution)/shard_map/reduce_sum | solution.py:94
  97.7 40.7 %all-reduce.12 = (f32[2]{0:T(128)S(1)}, f32[2]{0:T(128)S(1)}) all-reduce(f32[2]{0:T(128)S(1)} %get-tuple-element.8, f32[2]{0:T(128)S(1)} %get-tuple-element.7), channel_id=1, replica_groups=mesh['gx'=4,'gy'=8] {'gx','gy'}, use_global_device_ids=true, to_apply=%region_1.2 | all-reduce | flops 4 | bytes 32 | tf_op jit(solution)/shard_map/psum | solution.py:98
  138.5 1.6 broadcast_divide_fusion.1
  140.1 1.7 fusion.76
  141.7 1.6 copy.147
  143.3 1.3 collective-permute-start.12
  144.6 1.6 copy.149
  146.1 1.5 collective-permute-start.13
  147.6 1.4 copy.148
  149.0 2.7 collective-permute-done.13
  151.7 1.4 copy.150
  154.1 2.5 collective-permute-start.14
  156.6 1.6 collective-permute-start.15
  158.3 4.2 %collective-permute-done.15 = f32[2,7,130,1]{2,1,3,0:T(8,128)S(1)} collective-permute-done((f32[2,7,130,1]{2,1,3,0:T(8,128)S(1)}, f32[2,7,130,1]{2,1,3,0:T(8,128)S(1)}, u32[]{:S(2)}, u32[]{:S(2)}) %collective-permute-start.15) | collective-permute-done | bytes 7312 | tf_op jit(solution)/shard_map/ppermute | solution.py:23
  162.6 3.2 %multiply_reduce_fusion.1 = (f32[2]{0:T(128)S(1)}, f32[2]{0:T(128)S(1)}, f32[2,7,128,128]{2,1,3,0:T(8,128)}) fusion(f32[2,7,128,128]{2,1,3,0:T(8,128)S(1)} %broadcast_divide_fusion.1, f32[2,7,128,128]{2,1,3,0:T(8,128)S(1)} %get-tuple-element.25, f32[2,7,128,128]{2,1,3,0:T(8,128)S(1)} %copy-done.3, f32[2]{0:T(128)S(1)} %div.43, ...), kind=kLoop, calls=%fused_computation.98 | loop fusion | flops 6651900 | bytes 6779128 | tf_op jit(solution)/shard_map/reduce_sum | solution.py:94
  165.7 42.0 %all-reduce.11 = (f32[2]{0:T(128)S(1)}, f32[2]{0:T(128)S(1)}) all-reduce(f32[2]{0:T(128)S(1)} %get-tuple-element.6, f32[2]{0:T(128)S(1)} %get-tuple-element.5), channel_id=1, replica_groups=mesh['gx'=4,'gy'=8] {'gx','gy'}, use_global_device_ids=true, to_apply=%region_5.6 | all-reduce | flops 4 | bytes 32 | tf_op jit(solution)/shard_map/psum | solution.py:98
  207.7 3.4 %broadcast_divide_fusion = (f32[2,7,128,128]{2,1,3,0:T(8,128)S(1)}, f32[2,7,128,128]{2,1,3,0:T(8,128)}) fusion(f32[7,128,128]{1,0,2:T(8,128)} %copy.139, f32[2,7,128,128]{2,1,3,0:T(8,128)} %get-tuple-element.22, f32[2,7,128,128]{2,1,3,0:T(8,128)} %get-tuple-element.23, f32[2]{0:T(128)S(1)} %get-tuple-element.21, f32[2]{0:T(128)S(1)} %get-tuple-element.19, ...), kind=kLoop, calls=%fused_computation.103 | loop fusion | flops 1605632 | bytes 5046296 | tf_op jit(solution)/shard_map/div | solution.py:133
  211.1 1.7 fusion.75
  212.7 1.6 copy.153
  214.3 1.6 copy.155
  215.9 1.3 collective-permute-start.17
  217.2 3.0 %collective-permute-start.16 = (f32[2,7,1,128]{3,1,2,0:T(8,128)S(1)}, f32[2,7,1,128]{3,1,2,0:T(8,128)S(1)}, u32[]{:S(2)}, u32[]{:S(2)}) collective-permute-start(f32[2,7,1,128]{3,1,2,0:T(8,128)S(1)} %copy.153), channel_id=1, source_target_pairs={{0,8},{8,16},{16,24},{1,9},{9,17},{17,25},{2,10},{10,18},{18,26},{... | collective-permute-start | bytes 21512 | tf_op jit(solution)/shard_map/ppermute | solution.py:22
  220.2 2.2 fusion
  222.4 1.4 copy.154
  223.7 1.4 copy.156
  226.1 4.2 %collective-permute-start.18 = (f32[2,7,130,1]{2,1,3,0:T(8,128)S(1)}, f32[2,7,130,1]{2,1,3,0:T(8,128)S(1)}, u32[]{:S(2)}, u32[]{:S(2)}) collective-permute-start(f32[2,7,130,1]{2,1,3,0:T(8,128)S(1)} %get-tuple-element.31), channel_id=1, source_target_pairs={{0,1},{1,2},{2,3},{3,4},{4,5},{5,6},{6,7},{8,9},{9,10},{10,11},{11... | collective-permute-start | bytes 21848 | tf_op jit(solution)/shard_map/ppermute | solution.py:22
  230.3 1.3 collective-permute-start.19
  231.9 4.0 %collective-permute-done.19 = f32[2,7,130,1]{2,1,3,0:T(8,128)S(1)} collective-permute-done((f32[2,7,130,1]{2,1,3,0:T(8,128)S(1)}, f32[2,7,130,1]{2,1,3,0:T(8,128)S(1)}, u32[]{:S(2)}, u32[]{:S(2)}) %collective-permute-start.19) | collective-permute-done | bytes 7312 | tf_op jit(solution)/shard_map/ppermute | solution.py:23
  235.9 4.1 %fusion.7 = f32[2]{0:T(128)S(1)} fusion(f32[2,7,128,128]{2,1,3,0:T(8,128)S(1)} %get-tuple-element.17, f32[2,7,130,1]{2,1,3,0:T(8,128)S(1)} %collective-permute-done.19, f32[2,7,1,128]{2,1,3,0:T(8,128)} %copy.156, f32[2,7,1,128]{2,1,3,0:T(8,128)} %copy.154, f32[2,7,130,1]{2,1,3,0:T(8,128)S(1)} %collective-permute-done.18, f32[2,6,128,128]{2,1,3,0:T(8,128)} %fusion, ...), kind=kLoop, calls=%fused_computation.9 | loop fusion | flops 5734398 | bytes 4026600 | tf_op jit(solution)/shard_map/reduce_sum | solution.py:94
  240.0 40.4 %all-reduce.10 = (f32[2]{0:T(128)S(1)}, f32[2]{0:T(128)S(1)}) all-reduce(f32[2]{0:T(128)S(1)} %multiply_reduce_fusion, f32[2]{0:T(128)S(1)} %fusion.7), channel_id=1, replica_groups=mesh['gx'=4,'gy'=8] {'gx','gy'}, use_global_device_ids=true, to_apply=%region_9.10 | all-reduce | flops 4 | bytes 32 | tf_op jit(solution)/shard_map/psum | solution.py:98
  280.4 2.1 multiply_add_fusion
  282.5 1.3 copy.159
  (149 shorter events, 19.9 us)
Async XLA Ops:
  1.5 37.4 %collective-permute-start.3 = (f32[2,7,1,128]{3,1,2,0:T(8,128)}, f32[2,7,1,128]{3,1,2,0:T(8,128)S(1)}, u32[]{:S(2)}, u32[]{:S(2)}) collective-permute-start(f32[2,7,1,128]{3,1,2,0:T(8,128)} %copy.161), channel_id=1, source_target_pairs={{8,0},{16,8},{24,16},{9,1},{17,9},{25,17},{10,2},{18,10},{26,18},{... | collective-permute-start | bytes 21512 | tf_op jit(solution)/shard_map/ppermute | solution.py:23
  3.3 4.8 %copy-start.38 = (s32[3,128,128]{2,1,0:T(8,128)S(1)}, s32[3,128,128]{2,1,0:T(8,128)}, u32[]{:S(2)}) copy-start(s32[3,128,128]{2,1,0:T(8,128)} %param.8) | copy-start | bytes 589828
  3.3 34.5 %collective-permute-start.1 = (f32[2,7,1,128]{3,1,2,0:T(8,128)}, f32[2,7,1,128]{3,1,2,0:T(8,128)}, u32[]{:S(2)}, u32[]{:S(2)}) collective-permute-start(f32[2,7,1,128]{3,1,2,0:T(8,128)} %copy.160), channel_id=1, source_target_pairs={{0,8},{8,16},{16,24},{1,9},{9,17},{17,25},{2,10},{10,18},{18,26},{... | collective-permute-start | bytes 21512 | tf_op jit(solution)/shard_map/ppermute | solution.py:22
  8.1 7.4 %copy-start.32 = (f32[2,7,128,128]{3,2,1,0:T(8,128)S(1)}, f32[2,7,128,128]{3,2,1,0:T(8,128)}, u32[]{:S(2)}) copy-start(f32[2,7,128,128]{3,2,1,0:T(8,128)} %param.5) | copy-start | bytes 2752516
  8.4 6.5 %copy-start.34 = (f32[6,128,128]{2,1,0:T(8,128)}, f32[6,128,128]{2,1,0:T(8,128)S(1)}, u32[]{:S(2)}) copy-start(f32[6,128,128]{2,1,0:T(8,128)S(1)} %get-tuple-element.58) | copy-start | bytes 1179652
  8.4 6.5 %copy-start.36 = (f32[6,128,128]{2,1,0:T(8,128)}, f32[6,128,128]{2,1,0:T(8,128)S(1)}, u32[]{:S(2)}) copy-start(f32[6,128,128]{2,1,0:T(8,128)S(1)} %get-tuple-element.57) | copy-start | bytes 1179652
  8.4 21.0 %copy-start.29 = (f32[7,128,128]{2,1,0:T(8,128)}, f32[7,128,128]{2,1,0:T(8,128)S(1)}, u32[]{:S(2)}) copy-start(f32[7,128,128]{2,1,0:T(8,128)S(1)} %get-tuple-element.56) | copy-start | bytes 1376260
  9.0 20.4 %collective-permute-start.2 = (f32[7,1,128]{2,1,0:T(1,128)}, f32[7,1,128]{2,1,0:T(1,128)S(1)}, u32[]{:S(2)}, u32[]{:S(2)}) collective-permute-start(f32[7,1,128]{2,1,0:T(1,128)} %get-tuple-element.54), channel_id=1, source_target_pairs={{8,0},{16,8},{24,16},{9,1},{17,9},{25,17},{10,2},{18,10},{26,18},{... | collective-permute-start | bytes 10760 | tf_op jit(solution)/shard_map/ppermute | solution.py:23
  10.3 19.1 %collective-permute-start = (f32[7,1,128]{2,1,0:T(1,128)}, f32[7,1,128]{2,1,0:T(1,128)S(1)}, u32[]{:S(2)}, u32[]{:S(2)}) collective-permute-start(f32[7,1,128]{2,1,0:T(1,128)} %get-tuple-element.55), channel_id=1, source_target_pairs={{0,8},{8,16},{16,24},{1,9},{9,17},{17,25},{2,10},{10,18},{18,26},{... | collective-permute-start | bytes 10760 | tf_op jit(solution)/shard_map/ppermute | solution.py:22
  15.9 52.3 %copy-start = (f32[2,7,128,128]{2,1,3,0:T(8,128)}, f32[2,7,128,128]{2,1,3,0:T(8,128)S(1)}, u32[]{:S(2)}) copy-start(f32[2,7,128,128]{2,1,3,0:T(8,128)S(1)} %copy.146) | copy-start | bytes 2752516
  17.3 2.5 copy-start.35
  22.9 1.0 copy-start.37
  23.9 0.8 copy-start.4
  29.4 0.6 copy-start.39
  31.1 15.4 %collective-permute-start.6 = (f32[7,130,1]{2,1,0:T(8,128)}, f32[7,130,1]{2,1,0:T(8,128)}, u32[]{:S(2)}, u32[]{:S(2)}) collective-permute-start(f32[7,130,1]{2,1,0:T(8,128)} %get-tuple-element.51), channel_id=1, source_target_pairs={{1,0},{2,1},{3,2},{4,3},{5,4},{6,5},{7,6},{9,8},{10,9},{11,10},{12... | collective-permute-start | bytes 10928 | tf_op jit(solution)/shard_map/ppermute | solution.py:23
  32.4 25.6 %collective-permute-start.4 = (f32[7,130,1]{2,1,0:T(8,128)}, f32[7,130,1]{2,1,0:T(8,128)}, u32[]{:S(2)}, u32[]{:S(2)}) collective-permute-start(f32[7,130,1]{2,1,0:T(8,128)} %get-tuple-element.52), channel_id=1, source_target_pairs={{0,1},{1,2},{2,3},{3,4},{4,5},{5,6},{6,7},{8,9},{9,10},{10,11},{11... | collective-permute-start | bytes 10928 | tf_op jit(solution)/shard_map/ppermute | solution.py:22
  38.9 1.2 copy-start.25
  39.3 1.0 copy-start.26
  39.3 18.7 %copy-start.30 = (f32[7,128,128]{2,1,0:T(8,128)S(1)}, f32[7,128,128]{2,1,0:T(8,128)}, u32[]{:S(2)}) copy-start(f32[7,128,128]{2,1,0:T(8,128)} %copy-done.29) | copy-start | bytes 1376260
  39.3 18.7 %copy-start.33 = (f32[7,128,128]{2,1,0:T(8,128)S(1)}, f32[7,128,128]{2,1,0:T(8,128)}, u32[]{:S(2)}) copy-start(f32[7,128,128]{2,1,0:T(8,128)} %constant_dynamic-update-slice_fusion) | copy-start | bytes 1376260
  39.3 18.7 %copy-start.42 = (f32[7,1,128]{2,1,0:T(1,128)S(1)}, f32[7,1,128]{2,1,0:T(1,128)}, u32[]{:S(2)}) copy-start(f32[7,1,128]{2,1,0:T(1,128)} %copy-done.41) | copy-start | bytes 10756
  39.4 18.7 %copy-start.43 = (f32[7]{0:T(128)S(1)}, f32[7]{0:T(128)}, u32[]{:S(2)}) copy-start(f32[7]{0:T(128)} %constant.10.clone) | copy-start | bytes 88
  40.3 17.7 %copy-start.40 = (f32[7,1,128]{2,1,0:T(1,128)S(1)}, f32[7,1,128]{2,1,0:T(1,128)}, u32[]{:S(2)}) copy-start(f32[7,1,128]{2,1,0:T(1,128)} %copy-done.39) | copy-start | bytes 10756
  40.3 27.9 %collective-permute-start.5 = (f32[2,7,130,1]{2,1,3,0:T(8,128)}, f32[2,7,130,1]{2,1,3,0:T(8,128)S(1)}, u32[]{:S(2)}, u32[]{:S(2)}) collective-permute-start(f32[2,7,130,1]{2,1,3,0:T(8,128)} %get-tuple-element.37), channel_id=1, source_target_pairs={{0,1},{1,2},{2,3},{3,4},{4,5},{5,6},{6,7},{8,9},{9,10},{10,11},{11... | collective-permute-start | bytes 21848 | tf_op jit(solution)/shard_map/ppermute | solution.py:22
  44.0 24.3 %collective-permute-start.7 = (f32[2,7,130,1]{2,1,3,0:T(8,128)}, f32[2,7,130,1]{2,1,3,0:T(8,128)}, u32[]{:S(2)}, u32[]{:S(2)}) collective-permute-start(f32[2,7,130,1]{2,1,3,0:T(8,128)} %get-tuple-element.38), channel_id=1, source_target_pairs={{1,0},{2,1},{3,2},{4,3},{5,4},{6,5},{7,6},{9,8},{10,9},{11,10},{12... | collective-permute-start | bytes 21848 | tf_op jit(solution)/shard_map/ppermute | solution.py:23
  61.0 2.1 copy-start.31
  67.2 1.1 copy-start.44
  73.6 88.9 %copy-start.1 = (f32[2,7,128,128]{2,1,3,0:T(8,128)}, f32[2,7,128,128]{2,1,3,0:T(8,128)S(1)}, u32[]{:S(2)}) copy-start(f32[2,7,128,128]{2,1,3,0:T(8,128)S(1)} %get-tuple-element.25) | copy-start | bytes 2752516
  76.5 3.8 %collective-permute-start.8 = (f32[2,7,1,128]{3,1,2,0:T(8,128)S(1)}, f32[2,7,1,128]{3,1,2,0:T(8,128)S(1)}, u32[]{:S(2)}, u32[]{:S(2)}) collective-permute-start(f32[2,7,1,128]{3,1,2,0:T(8,128)S(1)} %copy.140), channel_id=1, source_target_pairs={{0,8},{8,16},{16,24},{1,9},{9,17},{17,25},{2,10},{10,18},{18,26},{... | collective-permute-start | bytes 21512 | tf_op jit(solution)/shard_map/ppermute | solution.py:22
  79.0 3.1 %collective-permute-start.9 = (f32[2,7,1,128]{3,1,2,0:T(8,128)S(1)}, f32[2,7,1,128]{3,1,2,0:T(8,128)S(1)}, u32[]{:S(2)}, u32[]{:S(2)}) collective-permute-start(f32[2,7,1,128]{3,1,2,0:T(8,128)S(1)} %copy.142), channel_id=1, source_target_pairs={{8,0},{16,8},{24,16},{9,1},{17,9},{25,17},{10,2},{18,10},{26,18},{... | collective-permute-start | bytes 21512 | tf_op jit(solution)/shard_map/ppermute | solution.py:23
  83.4 6.9 %copy-start.5 = (f32[6,128,128]{1,0,2:T(8,128)S(1)}, f32[6,128,128]{1,0,2:T(8,128)}, u32[]{:S(2)}) copy-start(f32[6,128,128]{1,0,2:T(8,128)} %copy-done.4) | copy-start | bytes 1179652
  83.4 11.2 %copy-start.23 = (f32[2,7,1,128]{2,1,3,0:T(8,128)S(1)}, f32[2,7,1,128]{2,1,3,0:T(8,128)}, u32[]{:S(2)}) copy-start(f32[2,7,1,128]{2,1,3,0:T(8,128)} %copy.143) | copy-start | bytes 21508
  84.4 6.1 %collective-permute-start.10 = (f32[2,7,130,1]{2,1,3,0:T(8,128)S(1)}, f32[2,7,130,1]{2,1,3,0:T(8,128)S(1)}, u32[]{:S(2)}, u32[]{:S(2)}) collective-permute-start(f32[2,7,130,1]{2,1,3,0:T(8,128)S(1)} %get-tuple-element.35), channel_id=1, source_target_pairs={{0,1},{1,2},{2,3},{3,4},{4,5},{5,6},{6,7},{8,9},{9,10},{10,11},{11... | collective-permute-start | bytes 21848 | tf_op jit(solution)/shard_map/ppermute | solution.py:22
  88.7 6.0 %copy-start.7 = (f32[7,128,128]{1,0,2:T(8,128)S(1)}, f32[7,128,128]{1,0,2:T(8,128)}, u32[]{:S(2)}) copy-start(f32[7,128,128]{1,0,2:T(8,128)} %copy.119) | copy-start | bytes 1376260
  88.7 6.0 %copy-start.10 = (f32[7,128,128]{1,0,2:T(8,128)S(1)}, f32[7,128,128]{1,0,2:T(8,128)}, u32[]{:S(2)}) copy-start(f32[7,128,128]{1,0,2:T(8,128)} %copy.124) | copy-start | bytes 1376260
  88.7 5.9 %copy-start.13 = (f32[7,128,128]{1,0,2:T(8,128)S(1)}, f32[7,128,128]{1,0,2:T(8,128)}, u32[]{:S(2)}) copy-start(f32[7,128,128]{1,0,2:T(8,128)} %copy.129) | copy-start | bytes 1376260
  88.7 5.9 %copy-start.16 = (f32[7,128,128]{1,0,2:T(8,128)S(1)}, f32[7,128,128]{1,0,2:T(8,128)}, u32[]{:S(2)}) copy-start(f32[7,128,128]{1,0,2:T(8,128)} %copy.134) | copy-start | bytes 1376260
  88.7 5.9 %copy-start.19 = (f32[7,128,128]{1,0,2:T(8,128)S(1)}, f32[7,128,128]{1,0,2:T(8,128)}, u32[]{:S(2)}) copy-start(f32[7,128,128]{1,0,2:T(8,128)} %copy.117) | copy-start | bytes 1376260
  88.7 5.9 %copy-start.22 = (f32[2,7,1,128]{2,1,3,0:T(8,128)S(1)}, f32[2,7,1,128]{2,1,3,0:T(8,128)}, u32[]{:S(2)}) copy-start(f32[2,7,1,128]{2,1,3,0:T(8,128)} %copy.141) | copy-start | bytes 21508
  88.7 5.9 %collective-permute-start.11 = (f32[2,7,130,1]{2,1,3,0:T(8,128)S(1)}, f32[2,7,130,1]{2,1,3,0:T(8,128)S(1)}, u32[]{:S(2)}, u32[]{:S(2)}) collective-permute-start(f32[2,7,130,1]{2,1,3,0:T(8,128)S(1)} %get-tuple-element.36), channel_id=1, source_target_pairs={{1,0},{2,1},{3,2},{4,3},{5,4},{6,5},{7,6},{9,8},{10,9},{11,10},{12... | collective-permute-start | bytes 21848 | tf_op jit(solution)/shard_map/ppermute | solution.py:23
  143.3 4.3 %collective-permute-start.12 = (f32[2,7,1,128]{3,1,2,0:T(8,128)S(1)}, f32[2,7,1,128]{3,1,2,0:T(8,128)S(1)}, u32[]{:S(2)}, u32[]{:S(2)}) collective-permute-start(f32[2,7,1,128]{3,1,2,0:T(8,128)S(1)} %copy.147), channel_id=1, source_target_pairs={{0,8},{8,16},{16,24},{1,9},{9,17},{17,25},{2,10},{10,18},{18,26},{... | collective-permute-start | bytes 21512 | tf_op jit(solution)/shard_map/ppermute | solution.py:22
  146.1 5.6 %collective-permute-start.13 = (f32[2,7,1,128]{3,1,2,0:T(8,128)S(1)}, f32[2,7,1,128]{3,1,2,0:T(8,128)S(1)}, u32[]{:S(2)}, u32[]{:S(2)}) collective-permute-start(f32[2,7,1,128]{3,1,2,0:T(8,128)S(1)} %copy.149), channel_id=1, source_target_pairs={{8,0},{16,8},{24,16},{9,1},{17,9},{25,17},{10,2},{18,10},{26,18},{... | collective-permute-start | bytes 21512 | tf_op jit(solution)/shard_map/ppermute | solution.py:23
  153.1 5.1 %copy-start.6 = (f32[6,128,128]{1,0,2:T(8,128)S(1)}, f32[6,128,128]{1,0,2:T(8,128)}, u32[]{:S(2)}) copy-start(f32[6,128,128]{1,0,2:T(8,128)} %copy-done.4) | copy-start | bytes 1179652
  153.1 9.4 %copy-start.27 = (f32[2,7,1,128]{2,1,3,0:T(8,128)S(1)}, f32[2,7,1,128]{2,1,3,0:T(8,128)}, u32[]{:S(2)}) copy-start(f32[2,7,1,128]{2,1,3,0:T(8,128)} %copy.148) | copy-start | bytes 21508
  153.1 9.4 %copy-start.28 = (f32[2,7,1,128]{2,1,3,0:T(8,128)S(1)}, f32[2,7,1,128]{2,1,3,0:T(8,128)}, u32[]{:S(2)}) copy-start(f32[2,7,1,128]{2,1,3,0:T(8,128)} %copy.150) | copy-start | bytes 21508
  154.1 4.3 %collective-permute-start.14 = (f32[2,7,130,1]{2,1,3,0:T(8,128)S(1)}, f32[2,7,130,1]{2,1,3,0:T(8,128)S(1)}, u32[]{:S(2)}, u32[]{:S(2)}) collective-permute-start(f32[2,7,130,1]{2,1,3,0:T(8,128)S(1)} %get-tuple-element.33), channel_id=1, source_target_pairs={{0,1},{1,2},{2,3},{3,4},{4,5},{5,6},{6,7},{8,9},{9,10},{10,11},{11... | collective-permute-start | bytes 21848 | tf_op jit(solution)/shard_map/ppermute | solution.py:22
  156.5 6.0 %copy-start.3 = (f32[2,7,128,128]{2,1,3,0:T(8,128)S(1)}, f32[2,7,128,128]{2,1,3,0:T(8,128)}, u32[]{:S(2)}) copy-start(f32[2,7,128,128]{2,1,3,0:T(8,128)} %get-tuple-element.23) | copy-start | bytes 2752516
  156.6 6.0 %copy-start.8 = (f32[7,128,128]{1,0,2:T(8,128)S(1)}, f32[7,128,128]{1,0,2:T(8,128)}, u32[]{:S(2)}) copy-start(f32[7,128,128]{1,0,2:T(8,128)} %copy.119) | copy-start | bytes 1376260
  156.6 6.0 %copy-start.11 = (f32[7,128,128]{1,0,2:T(8,128)S(1)}, f32[7,128,128]{1,0,2:T(8,128)}, u32[]{:S(2)}) copy-start(f32[7,128,128]{1,0,2:T(8,128)} %copy.124) | copy-start | bytes 1376260
  156.6 6.0 %copy-start.14 = (f32[7,128,128]{1,0,2:T(8,128)S(1)}, f32[7,128,128]{1,0,2:T(8,128)}, u32[]{:S(2)}) copy-start(f32[7,128,128]{1,0,2:T(8,128)} %copy.129) | copy-start | bytes 1376260
  156.6 6.0 %copy-start.17 = (f32[7,128,128]{1,0,2:T(8,128)S(1)}, f32[7,128,128]{1,0,2:T(8,128)}, u32[]{:S(2)}) copy-start(f32[7,128,128]{1,0,2:T(8,128)} %copy.134) | copy-start | bytes 1376260
  156.6 6.0 %copy-start.20 = (f32[7,128,128]{1,0,2:T(8,128)S(1)}, f32[7,128,128]{1,0,2:T(8,128)}, u32[]{:S(2)}) copy-start(f32[7,128,128]{1,0,2:T(8,128)} %copy.117) | copy-start | bytes 1376260
  156.6 5.9 %collective-permute-start.15 = (f32[2,7,130,1]{2,1,3,0:T(8,128)S(1)}, f32[2,7,130,1]{2,1,3,0:T(8,128)S(1)}, u32[]{:S(2)}, u32[]{:S(2)}) collective-permute-start(f32[2,7,130,1]{2,1,3,0:T(8,128)S(1)} %get-tuple-element.34), channel_id=1, source_target_pairs={{1,0},{2,1},{3,2},{4,3},{5,4},{6,5},{7,6},{9,8},{10,9},{11,10},{12... | collective-permute-start | bytes 21848 | tf_op jit(solution)/shard_map/ppermute | solution.py:23
  215.9 7.9 %collective-permute-start.17 = (f32[2,7,1,128]{3,1,2,0:T(8,128)S(1)}, f32[2,7,1,128]{3,1,2,0:T(8,128)S(1)}, u32[]{:S(2)}, u32[]{:S(2)}) collective-permute-start(f32[2,7,1,128]{3,1,2,0:T(8,128)S(1)} %copy.155), channel_id=1, source_target_pairs={{8,0},{16,8},{24,16},{9,1},{17,9},{25,17},{10,2},{18,10},{26,18},{... | collective-permute-start | bytes 21512 | tf_op jit(solution)/shard_map/ppermute | solution.py:23
  217.2 5.2 %collective-permute-start.16 = (f32[2,7,1,128]{3,1,2,0:T(8,128)S(1)}, f32[2,7,1,128]{3,1,2,0:T(8,128)S(1)}, u32[]{:S(2)}, u32[]{:S(2)}) collective-permute-start(f32[2,7,1,128]{3,1,2,0:T(8,128)S(1)} %copy.153), channel_id=1, source_target_pairs={{0,8},{8,16},{16,24},{1,9},{9,17},{17,25},{2,10},{10,18},{18,26},{... | collective-permute-start | bytes 21512 | tf_op jit(solution)/shard_map/ppermute | solution.py:22
  225.1 6.5 %copy-start.2 = (f32[7,128,128]{1,0,2:T(8,128)S(1)}, f32[7,128,128]{1,0,2:T(8,128)}, u32[]{:S(2)}) copy-start(f32[7,128,128]{1,0,2:T(8,128)} %copy.139) | copy-start | bytes 1376260
  225.1 6.5 %copy-start.24 = (f32[2,7,128,128]{2,1,3,0:T(8,128)S(1)}, f32[2,7,128,128]{2,1,3,0:T(8,128)}, u32[]{:S(2)}) copy-start(f32[2,7,128,128]{2,1,3,0:T(8,128)} %get-tuple-element.18) | copy-start | bytes 2752516
  225.1 10.8 %copy-start.18 = (f32[7,128,128]{1,0,2:T(8,128)S(1)}, f32[7,128,128]{1,0,2:T(8,128)}, u32[]{:S(2)}) copy-start(f32[7,128,128]{1,0,2:T(8,128)} %copy.134) | copy-start | bytes 1376260
  225.1 10.8 %copy-start.21 = (f32[7,128,128]{1,0,2:T(8,128)S(1)}, f32[7,128,128]{1,0,2:T(8,128)}, u32[]{:S(2)}) copy-start(f32[7,128,128]{1,0,2:T(8,128)} %copy.117) | copy-start | bytes 1376260
  226.1 5.8 %collective-permute-start.18 = (f32[2,7,130,1]{2,1,3,0:T(8,128)S(1)}, f32[2,7,130,1]{2,1,3,0:T(8,128)S(1)}, u32[]{:S(2)}, u32[]{:S(2)}) collective-permute-start(f32[2,7,130,1]{2,1,3,0:T(8,128)S(1)} %get-tuple-element.31), channel_id=1, source_target_pairs={{0,1},{1,2},{2,3},{3,4},{4,5},{5,6},{6,7},{8,9},{9,10},{10,11},{11... | collective-permute-start | bytes 21848 | tf_op jit(solution)/shard_map/ppermute | solution.py:22
  230.3 5.6 %collective-permute-start.19 = (f32[2,7,130,1]{2,1,3,0:T(8,128)S(1)}, f32[2,7,130,1]{2,1,3,0:T(8,128)S(1)}, u32[]{:S(2)}, u32[]{:S(2)}) collective-permute-start(f32[2,7,130,1]{2,1,3,0:T(8,128)S(1)} %get-tuple-element.32), channel_id=1, source_target_pairs={{1,0},{2,1},{3,2},{4,3},{5,4},{6,5},{7,6},{9,8},{10,9},{11,10},{12... | collective-permute-start | bytes 21848 | tf_op jit(solution)/shard_map/ppermute | solution.py:23
  231.6 4.3 %copy-start.9 = (f32[7,128,128]{1,0,2:T(8,128)S(1)}, f32[7,128,128]{1,0,2:T(8,128)}, u32[]{:S(2)}) copy-start(f32[7,128,128]{1,0,2:T(8,128)} %copy.119) | copy-start | bytes 1376260
  231.6 4.3 %copy-start.12 = (f32[7,128,128]{1,0,2:T(8,128)S(1)}, f32[7,128,128]{1,0,2:T(8,128)}, u32[]{:S(2)}) copy-start(f32[7,128,128]{1,0,2:T(8,128)} %copy.124) | copy-start | bytes 1376260
  231.6 4.3 %copy-start.15 = (f32[7,128,128]{1,0,2:T(8,128)S(1)}, f32[7,128,128]{1,0,2:T(8,128)}, u32[]{:S(2)}) copy-start(f32[7,128,128]{1,0,2:T(8,128)} %copy.129) | copy-start | bytes 1376260
  (1 other events, 0.6 us)
where the time goes:
time: 285 us; the launch traced here: 284 us
  blocking collectives  123 us (43%)
  starting transfers between devices  48.3 us (17%)
  local copies, waits for them, and re-layouts  47.9 us (17%)
  other arithmetic  35.5 us (12%)
  waiting for transfers between devices  28.2 us (10%)
    psum x3, blocking collectives, both_sums(): lax.psum((core_sum(residual, scaled), core_sum(scaled, image)), ('gx', 'g...  123 us
    ppermute x10, starting transfers between devices, extended_2(): before = lax.ppermute(last, axis, up)  34.7 us
    ppermute x10, waiting for transfers between devices, extended_2(): after = lax.ppermute(leading, axis, down)  16.7 us
    ppermute x10, starting transfers between devices, extended_2(): after = lax.ppermute(leading, axis, down)  13.6 us
    ppermute x10, waiting for transfers between devices, extended_2(): before = lax.ppermute(last, axis, up)  11.5 us
    reduce_sum x4, other arithmetic, core_sum(): return jnp.sum(first * second, axis=(1, 2, 3))  10.6 us
    div x3, other arithmetic, per_device(): scaled = residual / diagonal  10.3 us
    slice x7, local copies, waits for them, and re-layouts, extended_2(): last = lax.slice_in_dim(x, length - width, length, axis=dim)  10.2 us
  transfers between devices with their start and end apart: 20, of which 7 were waited for; matrix products, arithmetic and copies ran while one was open for 13% of the time, Pallas kernels for 0%

commit v1 on v0

--- a/solution.py
+++ b/solution.py
@@ -95,7 +95,7 @@
 
 
 def both_sums(residual, scaled, image):
-    return lax.psum((core_sum(residual, scaled), core_sum(scaled, image)), ("gx", "gy"))
+    return lax.psum(lax.psum((core_sum(residual, scaled), core_sum(scaled, image)), "gy"), "gx")
 
 
 def per_device(previous, dissipated, material, coolant):

time: 285 us -> 233 us (0.82)
  blocking collectives: 123 us -> 72.6 us
    psum x3 -> x6, blocking collectives: 123 us -> 72.6 us  [the longest x3 54.9 us: both_sums(): lax.psum((core_sum(residual, scaled), core_sum(scaled, image)), 'gy')]
  transfers between devices with their start and end apart: 20 -> 20, of which waited for: 7 -> 7; matrix products, arithmetic and copies ran while one was open for 13% -> 16% of each run, Pallas kernels for 0% -> 0%
where the time goes in v1:
time: 233 us; the launch traced here: 232 us
  blocking collectives  72.6 us (31%)
  local copies, waits for them, and re-layouts  48 us (21%)
  starting transfers between devices  47.5 us (20%)
  other arithmetic  35.5 us (15%)
  waiting for transfers between devices  27.1 us (12%)
    psum x3, blocking collectives, both_sums(): lax.psum((core_sum(residual, scaled), core_sum(scaled, image)), 'gy')  54.9 us
    ppermute x10, starting transfers between devices, extended_2(): before = lax.ppermute(last, axis, up)  33.9 us
    psum x3, blocking collectives, both_sums(): lax.psum(lax.psum((core_sum(residual, scaled), core_sum(scaled, image)),...  17.7 us
    ppermute x10, waiting for transfers between devices, extended_2(): after = lax.ppermute(leading, axis, down)  15.7 us
    ppermute x10, starting transfers between devices, extended_2(): after = lax.ppermute(leading, axis, down)  13.6 us
    ppermute x10, waiting for transfers between devices, extended_2(): before = lax.ppermute(last, axis, up)  11.5 us
    reduce_sum x4, other arithmetic, core_sum(): return jnp.sum(first * second, axis=(1, 2, 3))  10.6 us
    slice x7, local copies, waits for them, and re-layouts, extended_2(): last = lax.slice_in_dim(x, length - width, length, axis=dim)  10.2 us
  transfers between devices with their start and end apart: 20, of which 7 were waited for; matrix products, arithmetic and copies ran while one was open for 16% of the time, Pallas kernels for 0%

profile of v1, /device:TPU:0, one launch (start us, length us, event | category | flops | bytes accessed | tf_op | source)
XLA Modules:
  0.0 231.6 jit_solution(13868929208807221151)
XLA Ops:
  1.5 1.3 collective-permute-start.3
  3.3 3.7 %collective-permute-start.1 = (f32[2,7,1,128]{3,1,2,0:T(8,128)}, f32[2,7,1,128]{3,1,2,0:T(8,128)}, u32[]{:S(2)}, u32[]{:S(2)}) collective-permute-start(f32[2,7,1,128]{3,1,2,0:T(8,128)} %copy.160), channel_id=1, source_target_pairs={{0,8},{8,16},{16,24},{1,9},{9,17},{17,25},{2,10},{10,18},{18,26},{... | collective-permute-start | bytes 21512 | tf_op jit(solution)/shard_map/ppermute | solution.py:22
  9.0 1.3 collective-permute-start.2
  10.3 4.6 %collective-permute-start = (f32[7,1,128]{2,1,0:T(1,128)}, f32[7,1,128]{2,1,0:T(1,128)S(1)}, u32[]{:S(2)}, u32[]{:S(2)}) collective-permute-start(f32[7,1,128]{2,1,0:T(1,128)} %get-tuple-element.61), channel_id=1, source_target_pairs={{0,8},{8,16},{16,24},{1,9},{9,17},{17,25},{2,10},{10,18},{18,26},{... | collective-permute-start | bytes 10760 | tf_op jit(solution)/shard_map/ppermute | solution.py:22
  21.7 1.1 sqrt_multiply_fusion
  24.7 1.1 fusion.44
  27.0 2.5 %stack.15 = f32[2,7,128,128]{2,1,3,0:T(8,128)} concatenate(f32[2,1,128,128]{2,1,3,0:T(1,128)S(1)} %copy.113, f32[2,1,128,128]{2,1,3,0:T(1,128)S(1)} %broadcast.72, f32[2,1,128,128]{2,1,3,0:T(1,128)S(1)} %copy.114, f32[2,1,128,128]{2,1,3,0:T(1,128)S(1)} %broadcast.72, f32[2,1,128,128]{2,1,3,0:T(1,128)S(1)} %copy.115, f32[2,1,128,128]{2,1,3,0:T(1,128)S(1)} %broadcast.72, ...), dimensions={1} | concatenate | bytes 1835008 | tf_op jit(solution)/shard_map/stack | solution.py:48
  30.0 1.1 fusion.80
  31.1 1.3 collective-permute-start.6
  32.4 5.3 %collective-permute-start.4 = (f32[7,130,1]{2,1,0:T(8,128)}, f32[7,130,1]{2,1,0:T(8,128)}, u32[]{:S(2)}, u32[]{:S(2)}) collective-permute-start(f32[7,130,1]{2,1,0:T(8,128)} %get-tuple-element.58), channel_id=1, source_target_pairs={{0,1},{1,2},{2,3},{3,4},{4,5},{5,6},{6,7},{8,9},{9,10},{10,11},{11... | collective-permute-start | bytes 10928 | tf_op jit(solution)/shard_map/ppermute | solution.py:22
  37.8 1.1 copy.121
  40.3 3.6 %collective-permute-start.5 = (f32[2,7,130,1]{2,1,3,0:T(8,128)}, f32[2,7,130,1]{2,1,3,0:T(8,128)S(1)}, u32[]{:S(2)}, u32[]{:S(2)}) collective-permute-start(f32[2,7,130,1]{2,1,3,0:T(8,128)} %get-tuple-element.43), channel_id=1, source_target_pairs={{0,1},{1,2},{2,3},{3,4},{4,5},{5,6},{6,7},{8,9},{9,10},{10,11},{11... | collective-permute-start | bytes 21848 | tf_op jit(solution)/shard_map/ppermute | solution.py:22
  44.0 1.3 collective-permute-start.7
  45.3 1.3 collective-permute-done.6
  46.6 11.4 %collective-permute-done.4 = f32[7,130,1]{2,1,0:T(8,128)} collective-permute-done((f32[7,130,1]{2,1,0:T(8,128)}, f32[7,130,1]{2,1,0:T(8,128)}, u32[]{:S(2)}, u32[]{:S(2)}) %collective-permute-start.4) | collective-permute-done | bytes 3672 | tf_op jit(solution)/shard_map/ppermute | solution.py:22
  58.0 3.0 %add_add_fusion = (f32[7,128,128]{2,1,0:T(8,128)}, f32[7,128,128]{2,1,0:T(8,128)}, f32[7,128,128]{2,1,0:T(8,128)S(1)}, f32[7,128,128]{2,1,0:T(8,128)S(1)}, f32[7...) fusion(f32[6,128,128]{2,1,0:T(8,128)S(1)} %sqrt_multiply_fusion, f32[7,128,128]{2,1,0:T(8,128)S(1)} %copy-done.33, ...), kind=kLoop, calls=%fused_computation.123 | loop fusion | flops 2179072 | bytes 4077708 | tf_op jit(solution)/shard_map/add | solution.py:90
  61.0 2.1 copy.139
  66.2 1.1 copy.134
  67.2 1.1 copy.117
  68.3 5.3 %broadcast_divide_fusion.2 = (f32[2,7,128,128]{2,1,3,0:T(8,128)S(1)}, f32[2,7,128,128]{2,1,3,0:T(8,128)S(1)}) fusion(f32[7,128,128]{1,0,2:T(8,128)} %copy.139, f32[2,6,128,128]{2,1,3,0:T(8,128)} %fusion.44, f32[2,7,128,128]{2,1,3,0:T(8,128)S(1)} %copy.146, f32[2,7,130,1]{2,1,3,0:T(8,128)} %collective-permute-done.7, f32[2,7,1,128]{2,1,3,0:T(8,128)} %copy-done.26, ...), kind=kLoop, calls=%fused_computation.105 | loop fusion | flops 6193152 | bytes 7237884 | tf_op jit(solution)/shard_map/div | solution.py:122
  73.6 1.3 fusion.77
  74.9 1.6 copy.140
  76.5 2.1 collective-permute-start.8
  78.9 1.3 collective-permute-start.9
  80.3 1.4 copy.141
  82.0 1.4 copy.143
  84.3 4.3 %collective-permute-start.10 = (f32[2,7,130,1]{2,1,3,0:T(8,128)S(1)}, f32[2,7,130,1]{2,1,3,0:T(8,128)S(1)}, u32[]{:S(2)}, u32[]{:S(2)}) collective-permute-start(f32[2,7,130,1]{2,1,3,0:T(8,128)S(1)} %get-tuple-element.41), channel_id=1, source_target_pairs={{0,1},{1,2},{2,3},{3,4},{4,5},{5,6},{6,7},{8,9},{9,10},{10,11},{11... | collective-permute-start | bytes 21848 | tf_op jit(solution)/shard_map/ppermute | solution.py:22
  88.7 1.6 collective-permute-start.11
  90.4 4.2 %collective-permute-done.11 = f32[2,7,130,1]{2,1,3,0:T(8,128)S(1)} collective-permute-done((f32[2,7,130,1]{2,1,3,0:T(8,128)S(1)}, f32[2,7,130,1]{2,1,3,0:T(8,128)S(1)}, u32[]{:S(2)}, u32[]{:S(2)}) %collective-permute-start.11) | collective-permute-done | bytes 7312 | tf_op jit(solution)/shard_map/ppermute | solution.py:23
  94.6 3.1 %multiply_reduce_fusion.3 = (f32[2]{0:T(128)S(1)}, f32[2]{0:T(128)S(1)}, f32[2,7,128,128]{2,1,3,0:T(8,128)}) fusion(f32[2,7,128,128]{2,1,3,0:T(8,128)S(1)} %get-tuple-element.30, f32[2,7,128,128]{2,1,3,0:T(8,128)S(1)} %get-tuple-element.31, f32[2,6,128,128]{2,1,3,0:T(8,128)S(1)} %fusion.30, f32[2,7,130,1]{2,1,3,0:T(8,128)S(1)} %collective-permute-done.11, ...), kind=kLoop, calls=%fused_computation.101 | loop fusion | flops 6193148 | bytes 5861616 | tf_op jit(solution)/shard_map/reduce_sum | solution.py:94
  97.7 18.8 %all-reduce.12 = (f32[2]{0:T(128)S(1)}, f32[2]{0:T(128)S(1)}) all-reduce(f32[2]{0:T(128)S(1)} %get-tuple-element.8, f32[2]{0:T(128)S(1)} %get-tuple-element.7), channel_id=1, replica_groups=mesh['gx'=4,'gy'=8] {'gy'}, use_global_device_ids=true, to_apply=%region_1.2 | all-reduce | flops 4 | bytes 32 | tf_op jit(solution)/shard_map/psum | solution.py:98
  116.5 5.6 %all-reduce.15 = (f32[2]{0:T(128)S(1)}, f32[2]{0:T(128)S(1)}) all-reduce(f32[2]{0:T(128)S(1)} %get-tuple-element.13, f32[2]{0:T(128)S(1)} %get-tuple-element.14), channel_id=1, replica_groups=mesh['gx'=4,'gy'=8] {'gx'}, use_global_device_ids=true, to_apply=%region_2.3 | all-reduce | flops 4 | bytes 32 | tf_op jit(solution)/shard_map/psum | solution.py:98
  122.2 1.6 broadcast_divide_fusion.1
  123.8 1.7 fusion.76
  125.5 1.6 copy.147
  127.0 2.0 collective-permute-start.12
  129.0 1.6 copy.149
  130.6 1.3 collective-permute-start.13
  131.9 1.4 copy.148
  133.3 1.9 collective-permute-done.13
  135.1 1.4 copy.150
  137.5 2.2 collective-permute-start.14
  139.8 1.7 collective-permute-start.15
  141.7 4.0 %collective-permute-done.15 = f32[2,7,130,1]{2,1,3,0:T(8,128)S(1)} collective-permute-done((f32[2,7,130,1]{2,1,3,0:T(8,128)S(1)}, f32[2,7,130,1]{2,1,3,0:T(8,128)S(1)}, u32[]{:S(2)}, u32[]{:S(2)}) %collective-permute-start.15) | collective-permute-done | bytes 7312 | tf_op jit(solution)/shard_map/ppermute | solution.py:23
  145.7 3.2 %multiply_reduce_fusion.1 = (f32[2]{0:T(128)S(1)}, f32[2]{0:T(128)S(1)}, f32[2,7,128,128]{2,1,3,0:T(8,128)}) fusion(f32[2,7,128,128]{2,1,3,0:T(8,128)S(1)} %broadcast_divide_fusion.1, f32[2,7,128,128]{2,1,3,0:T(8,128)S(1)} %get-tuple-element.31, f32[2,7,128,128]{2,1,3,0:T(8,128)S(1)} %copy-done.3, f32[2]{0:T(128)S(1)} %div.43, ...), kind=kLoop, calls=%fused_computation.98 | loop fusion | flops 6651900 | bytes 6779128 | tf_op jit(solution)/shard_map/reduce_sum | solution.py:94
  148.9 18.0 %all-reduce.11 = (f32[2]{0:T(128)S(1)}, f32[2]{0:T(128)S(1)}) all-reduce(f32[2]{0:T(128)S(1)} %get-tuple-element.6, f32[2]{0:T(128)S(1)} %get-tuple-element.5), channel_id=1, replica_groups=mesh['gx'=4,'gy'=8] {'gy'}, use_global_device_ids=true, to_apply=%region_7.8 | all-reduce | flops 4 | bytes 32 | tf_op jit(solution)/shard_map/psum | solution.py:98
  166.9 6.0 %all-reduce.14 = (f32[2]{0:T(128)S(1)}, f32[2]{0:T(128)S(1)}) all-reduce(f32[2]{0:T(128)S(1)} %get-tuple-element.11, f32[2]{0:T(128)S(1)} %get-tuple-element.12), channel_id=1, replica_groups=mesh['gx'=4,'gy'=8] {'gx'}, use_global_device_ids=true, to_apply=%region_8.9 | all-reduce | flops 4 | bytes 32 | tf_op jit(solution)/shard_map/psum | solution.py:98
  172.9 3.3 %broadcast_divide_fusion = (f32[2,7,128,128]{2,1,3,0:T(8,128)S(1)}, f32[2,7,128,128]{2,1,3,0:T(8,128)}) fusion(f32[7,128,128]{1,0,2:T(8,128)} %copy.139, f32[2,7,128,128]{2,1,3,0:T(8,128)} %get-tuple-element.28, f32[2,7,128,128]{2,1,3,0:T(8,128)} %get-tuple-element.29, f32[2]{0:T(128)S(1)} %get-tuple-element.27, f32[2]{0:T(128)S(1)} %get-tuple-element.25, ...), kind=kLoop, calls=%fused_computation.103 | loop fusion | flops 1605632 | bytes 5046296 | tf_op jit(solution)/shard_map/div | solution.py:133
  176.2 1.7 fusion.75
  177.9 1.6 copy.153
  179.5 1.6 copy.155
  181.0 1.3 collective-permute-start.17
  182.3 3.0 %collective-permute-start.16 = (f32[2,7,1,128]{3,1,2,0:T(8,128)S(1)}, f32[2,7,1,128]{3,1,2,0:T(8,128)S(1)}, u32[]{:S(2)}, u32[]{:S(2)}) collective-permute-start(f32[2,7,1,128]{3,1,2,0:T(8,128)S(1)} %copy.153), channel_id=1, source_target_pairs={{0,8},{8,16},{16,24},{1,9},{9,17},{17,25},{2,10},{10,18},{18,26},{... | collective-permute-start | bytes 21512 | tf_op jit(solution)/shard_map/ppermute | solution.py:22
  185.4 2.2 fusion
  187.5 1.4 copy.154
  188.9 1.4 copy.156
  191.3 3.0 %collective-permute-start.18 = (f32[2,7,130,1]{2,1,3,0:T(8,128)S(1)}, f32[2,7,130,1]{2,1,3,0:T(8,128)S(1)}, u32[]{:S(2)}, u32[]{:S(2)}) collective-permute-start(f32[2,7,130,1]{2,1,3,0:T(8,128)S(1)} %get-tuple-element.37), channel_id=1, source_target_pairs={{0,1},{1,2},{2,3},{3,4},{4,5},{5,6},{6,7},{8,9},{9,10},{10,11},{11... | collective-permute-start | bytes 21848 | tf_op jit(solution)/shard_map/ppermute | solution.py:22
  194.3 1.3 collective-permute-start.19
  195.9 4.0 %collective-permute-done.19 = f32[2,7,130,1]{2,1,3,0:T(8,128)S(1)} collective-permute-done((f32[2,7,130,1]{2,1,3,0:T(8,128)S(1)}, f32[2,7,130,1]{2,1,3,0:T(8,128)S(1)}, u32[]{:S(2)}, u32[]{:S(2)}) %collective-permute-start.19) | collective-permute-done | bytes 7312 | tf_op jit(solution)/shard_map/ppermute | solution.py:23
  199.9 4.1 %fusion.7 = f32[2]{0:T(128)S(1)} fusion(f32[2,7,128,128]{2,1,3,0:T(8,128)S(1)} %get-tuple-element.23, f32[2,7,130,1]{2,1,3,0:T(8,128)S(1)} %collective-permute-done.19, f32[2,7,1,128]{2,1,3,0:T(8,128)} %copy.156, f32[2,7,1,128]{2,1,3,0:T(8,128)} %copy.154, f32[2,7,130,1]{2,1,3,0:T(8,128)S(1)} %collective-permute-done.18, f32[2,6,128,128]{2,1,3,0:T(8,128)} %fusion, ...), kind=kLoop, calls=%fused_computation.9 | loop fusion | flops 5734398 | bytes 4026600 | tf_op jit(solution)/shard_map/reduce_sum | solution.py:94
  204.0 18.0 %all-reduce.10 = (f32[2]{0:T(128)S(1)}, f32[2]{0:T(128)S(1)}) all-reduce(f32[2]{0:T(128)S(1)} %multiply_reduce_fusion, f32[2]{0:T(128)S(1)} %fusion.7), channel_id=1, replica_groups=mesh['gx'=4,'gy'=8] {'gy'}, use_global_device_ids=true, to_apply=%region_13.14 | all-reduce | flops 4 | bytes 32 | tf_op jit(solution)/shard_map/psum | solution.py:98
  222.1 6.1 %all-reduce.13 = (f32[2]{0:T(128)S(1)}, f32[2]{0:T(128)S(1)}) all-reduce(f32[2]{0:T(128)S(1)} %get-tuple-element.9, f32[2]{0:T(128)S(1)} %get-tuple-element.10), channel_id=1, replica_groups=mesh['gx'=4,'gy'=8] {'gx'}, use_global_device_ids=true, to_apply=%region_14.15 | all-reduce | flops 4 | bytes 32 | tf_op jit(solution)/shard_map/psum | solution.py:98
  228.2 2.1 multiply_add_fusion
  230.4 1.3 copy.159
  (152 shorter events, 23.1 us)
Async XLA Ops:
  1.5 37.4 %collective-permute-start.3 = (f32[2,7,1,128]{3,1,2,0:T(8,128)}, f32[2,7,1,128]{3,1,2,0:T(8,128)S(1)}, u32[]{:S(2)}, u32[]{:S(2)}) collective-permute-start(f32[2,7,1,128]{3,1,2,0:T(8,128)} %copy.161), channel_id=1, source_target_pairs={{8,0},{16,8},{24,16},{9,1},{17,9},{25,17},{10,2},{18,10},{26,18},{... | collective-permute-start | bytes 21512 | tf_op jit(solution)/shard_map/ppermute | solution.py:23
  3.3 4.8 %copy-start.38 = (s32[3,128,128]{2,1,0:T(8,128)S(1)}, s32[3,128,128]{2,1,0:T(8,128)}, u32[]{:S(2)}) copy-start(s32[3,128,128]{2,1,0:T(8,128)} %param.8) | copy-start | bytes 589828
  3.3 34.4 %collective-permute-start.1 = (f32[2,7,1,128]{3,1,2,0:T(8,128)}, f32[2,7,1,128]{3,1,2,0:T(8,128)}, u32[]{:S(2)}, u32[]{:S(2)}) collective-permute-start(f32[2,7,1,128]{3,1,2,0:T(8,128)} %copy.160), channel_id=1, source_target_pairs={{0,8},{8,16},{16,24},{1,9},{9,17},{17,25},{2,10},{10,18},{18,26},{... | collective-permute-start | bytes 21512 | tf_op jit(solution)/shard_map/ppermute | solution.py:22
  8.1 7.4 %copy-start.32 = (f32[2,7,128,128]{3,2,1,0:T(8,128)S(1)}, f32[2,7,128,128]{3,2,1,0:T(8,128)}, u32[]{:S(2)}) copy-start(f32[2,7,128,128]{3,2,1,0:T(8,128)} %param.5) | copy-start | bytes 2752516
  8.4 6.5 %copy-start.34 = (f32[6,128,128]{2,1,0:T(8,128)}, f32[6,128,128]{2,1,0:T(8,128)S(1)}, u32[]{:S(2)}) copy-start(f32[6,128,128]{2,1,0:T(8,128)S(1)} %get-tuple-element.64) | copy-start | bytes 1179652
  8.4 6.5 %copy-start.36 = (f32[6,128,128]{2,1,0:T(8,128)}, f32[6,128,128]{2,1,0:T(8,128)S(1)}, u32[]{:S(2)}) copy-start(f32[6,128,128]{2,1,0:T(8,128)S(1)} %get-tuple-element.63) | copy-start | bytes 1179652
  8.4 21.0 %copy-start.29 = (f32[7,128,128]{2,1,0:T(8,128)}, f32[7,128,128]{2,1,0:T(8,128)S(1)}, u32[]{:S(2)}) copy-start(f32[7,128,128]{2,1,0:T(8,128)S(1)} %get-tuple-element.62) | copy-start | bytes 1376260
  9.0 20.4 %collective-permute-start.2 = (f32[7,1,128]{2,1,0:T(1,128)}, f32[7,1,128]{2,1,0:T(1,128)S(1)}, u32[]{:S(2)}, u32[]{:S(2)}) collective-permute-start(f32[7,1,128]{2,1,0:T(1,128)} %get-tuple-element.60), channel_id=1, source_target_pairs={{8,0},{16,8},{24,16},{9,1},{17,9},{25,17},{10,2},{18,10},{26,18},{... | collective-permute-start | bytes 10760 | tf_op jit(solution)/shard_map/ppermute | solution.py:23
  10.3 19.1 %collective-permute-start = (f32[7,1,128]{2,1,0:T(1,128)}, f32[7,1,128]{2,1,0:T(1,128)S(1)}, u32[]{:S(2)}, u32[]{:S(2)}) collective-permute-start(f32[7,1,128]{2,1,0:T(1,128)} %get-tuple-element.61), channel_id=1, source_target_pairs={{0,8},{8,16},{16,24},{1,9},{9,17},{17,25},{2,10},{10,18},{18,26},{... | collective-permute-start | bytes 10760 | tf_op jit(solution)/shard_map/ppermute | solution.py:22
  16.0 52.3 %copy-start = (f32[2,7,128,128]{2,1,3,0:T(8,128)}, f32[2,7,128,128]{2,1,3,0:T(8,128)S(1)}, u32[]{:S(2)}) copy-start(f32[2,7,128,128]{2,1,3,0:T(8,128)S(1)} %copy.146) | copy-start | bytes 2752516
  17.3 2.5 %copy-start.35 = (f32[6,128,128]{2,1,0:T(8,128)S(1)}, f32[6,128,128]{2,1,0:T(8,128)}, u32[]{:S(2)}) copy-start(f32[6,128,128]{2,1,0:T(8,128)} %slice_dynamic-update-slice_fusion.10) | copy-start | bytes 1179652
  22.9 1.0 copy-start.37
  23.9 0.8 copy-start.4
  29.5 0.6 copy-start.41
  31.1 15.4 %collective-permute-start.6 = (f32[7,130,1]{2,1,0:T(8,128)}, f32[7,130,1]{2,1,0:T(8,128)}, u32[]{:S(2)}, u32[]{:S(2)}) collective-permute-start(f32[7,130,1]{2,1,0:T(8,128)} %get-tuple-element.57), channel_id=1, source_target_pairs={{1,0},{2,1},{3,2},{4,3},{5,4},{6,5},{7,6},{9,8},{10,9},{11,10},{12... | collective-permute-start | bytes 10928 | tf_op jit(solution)/shard_map/ppermute | solution.py:23
  32.4 25.6 %collective-permute-start.4 = (f32[7,130,1]{2,1,0:T(8,128)}, f32[7,130,1]{2,1,0:T(8,128)}, u32[]{:S(2)}, u32[]{:S(2)}) collective-permute-start(f32[7,130,1]{2,1,0:T(8,128)} %get-tuple-element.58), channel_id=1, source_target_pairs={{0,1},{1,2},{2,3},{3,4},{4,5},{5,6},{6,7},{8,9},{9,10},{10,11},{11... | collective-permute-start | bytes 10928 | tf_op jit(solution)/shard_map/ppermute | solution.py:22
  38.8 1.2 copy-start.25
  39.3 1.0 copy-start.26
  39.3 18.7 %copy-start.30 = (f32[7,128,128]{2,1,0:T(8,128)S(1)}, f32[7,128,128]{2,1,0:T(8,128)}, u32[]{:S(2)}) copy-start(f32[7,128,128]{2,1,0:T(8,128)} %copy-done.29) | copy-start | bytes 1376260
  39.3 18.7 %copy-start.33 = (f32[7,128,128]{2,1,0:T(8,128)S(1)}, f32[7,128,128]{2,1,0:T(8,128)}, u32[]{:S(2)}) copy-start(f32[7,128,128]{2,1,0:T(8,128)} %constant_dynamic-update-slice_fusion) | copy-start | bytes 1376260
  39.3 18.7 %copy-start.42 = (f32[7,1,128]{2,1,0:T(1,128)S(1)}, f32[7,1,128]{2,1,0:T(1,128)}, u32[]{:S(2)}) copy-start(f32[7,1,128]{2,1,0:T(1,128)} %copy-done.41) | copy-start | bytes 10756
  39.3 18.7 %copy-start.43 = (f32[7]{0:T(128)S(1)}, f32[7]{0:T(128)}, u32[]{:S(2)}) copy-start(f32[7]{0:T(128)} %constant.10.clone) | copy-start | bytes 88
  40.3 17.7 %copy-start.40 = (f32[7,1,128]{2,1,0:T(1,128)S(1)}, f32[7,1,128]{2,1,0:T(1,128)}, u32[]{:S(2)}) copy-start(f32[7,1,128]{2,1,0:T(1,128)} %copy-done.39) | copy-start | bytes 10756
  40.3 28.0 %collective-permute-start.5 = (f32[2,7,130,1]{2,1,3,0:T(8,128)}, f32[2,7,130,1]{2,1,3,0:T(8,128)S(1)}, u32[]{:S(2)}, u32[]{:S(2)}) collective-permute-start(f32[2,7,130,1]{2,1,3,0:T(8,128)} %get-tuple-element.43), channel_id=1, source_target_pairs={{0,1},{1,2},{2,3},{3,4},{4,5},{5,6},{6,7},{8,9},{9,10},{10,11},{11... | collective-permute-start | bytes 21848 | tf_op jit(solution)/shard_map/ppermute | solution.py:22
  44.0 24.3 %collective-permute-start.7 = (f32[2,7,130,1]{2,1,3,0:T(8,128)}, f32[2,7,130,1]{2,1,3,0:T(8,128)}, u32[]{:S(2)}, u32[]{:S(2)}) collective-permute-start(f32[2,7,130,1]{2,1,3,0:T(8,128)} %get-tuple-element.44), channel_id=1, source_target_pairs={{1,0},{2,1},{3,2},{4,3},{5,4},{6,5},{7,6},{9,8},{10,9},{11,10},{12... | collective-permute-start | bytes 21848 | tf_op jit(solution)/shard_map/ppermute | solution.py:23
  61.0 2.1 copy-start.31
  67.2 1.1 copy-start.44
  73.6 72.1 %copy-start.1 = (f32[2,7,128,128]{2,1,3,0:T(8,128)}, f32[2,7,128,128]{2,1,3,0:T(8,128)S(1)}, u32[]{:S(2)}) copy-start(f32[2,7,128,128]{2,1,3,0:T(8,128)S(1)} %get-tuple-element.31) | copy-start | bytes 2752516
  76.5 3.8 %collective-permute-start.8 = (f32[2,7,1,128]{3,1,2,0:T(8,128)S(1)}, f32[2,7,1,128]{3,1,2,0:T(8,128)S(1)}, u32[]{:S(2)}, u32[]{:S(2)}) collective-permute-start(f32[2,7,1,128]{3,1,2,0:T(8,128)S(1)} %copy.140), channel_id=1, source_target_pairs={{0,8},{8,16},{16,24},{1,9},{9,17},{17,25},{2,10},{10,18},{18,26},{... | collective-permute-start | bytes 21512 | tf_op jit(solution)/shard_map/ppermute | solution.py:22
  78.9 3.1 %collective-permute-start.9 = (f32[2,7,1,128]{3,1,2,0:T(8,128)S(1)}, f32[2,7,1,128]{3,1,2,0:T(8,128)S(1)}, u32[]{:S(2)}, u32[]{:S(2)}) collective-permute-start(f32[2,7,1,128]{3,1,2,0:T(8,128)S(1)} %copy.142), channel_id=1, source_target_pairs={{8,0},{16,8},{24,16},{9,1},{17,9},{25,17},{10,2},{18,10},{26,18},{... | collective-permute-start | bytes 21512 | tf_op jit(solution)/shard_map/ppermute | solution.py:23
  83.4 6.9 %copy-start.5 = (f32[6,128,128]{1,0,2:T(8,128)S(1)}, f32[6,128,128]{1,0,2:T(8,128)}, u32[]{:S(2)}) copy-start(f32[6,128,128]{1,0,2:T(8,128)} %copy-done.4) | copy-start | bytes 1179652
  83.4 11.2 %copy-start.23 = (f32[2,7,1,128]{2,1,3,0:T(8,128)S(1)}, f32[2,7,1,128]{2,1,3,0:T(8,128)}, u32[]{:S(2)}) copy-start(f32[2,7,1,128]{2,1,3,0:T(8,128)} %copy.143) | copy-start | bytes 21508
  84.3 6.1 %collective-permute-start.10 = (f32[2,7,130,1]{2,1,3,0:T(8,128)S(1)}, f32[2,7,130,1]{2,1,3,0:T(8,128)S(1)}, u32[]{:S(2)}, u32[]{:S(2)}) collective-permute-start(f32[2,7,130,1]{2,1,3,0:T(8,128)S(1)} %get-tuple-element.41), channel_id=1, source_target_pairs={{0,1},{1,2},{2,3},{3,4},{4,5},{5,6},{6,7},{8,9},{9,10},{10,11},{11... | collective-permute-start | bytes 21848 | tf_op jit(solution)/shard_map/ppermute | solution.py:22
  88.6 6.0 %copy-start.7 = (f32[7,128,128]{1,0,2:T(8,128)S(1)}, f32[7,128,128]{1,0,2:T(8,128)}, u32[]{:S(2)}) copy-start(f32[7,128,128]{1,0,2:T(8,128)} %copy.119) | copy-start | bytes 1376260
  88.7 6.0 %copy-start.10 = (f32[7,128,128]{1,0,2:T(8,128)S(1)}, f32[7,128,128]{1,0,2:T(8,128)}, u32[]{:S(2)}) copy-start(f32[7,128,128]{1,0,2:T(8,128)} %copy.124) | copy-start | bytes 1376260
  88.7 5.9 %copy-start.13 = (f32[7,128,128]{1,0,2:T(8,128)S(1)}, f32[7,128,128]{1,0,2:T(8,128)}, u32[]{:S(2)}) copy-start(f32[7,128,128]{1,0,2:T(8,128)} %copy.129) | copy-start | bytes 1376260
  88.7 5.9 %copy-start.16 = (f32[7,128,128]{1,0,2:T(8,128)S(1)}, f32[7,128,128]{1,0,2:T(8,128)}, u32[]{:S(2)}) copy-start(f32[7,128,128]{1,0,2:T(8,128)} %copy.134) | copy-start | bytes 1376260
  88.7 5.9 %copy-start.19 = (f32[7,128,128]{1,0,2:T(8,128)S(1)}, f32[7,128,128]{1,0,2:T(8,128)}, u32[]{:S(2)}) copy-start(f32[7,128,128]{1,0,2:T(8,128)} %copy.117) | copy-start | bytes 1376260
  88.7 5.9 %copy-start.22 = (f32[2,7,1,128]{2,1,3,0:T(8,128)S(1)}, f32[2,7,1,128]{2,1,3,0:T(8,128)}, u32[]{:S(2)}) copy-start(f32[2,7,1,128]{2,1,3,0:T(8,128)} %copy.141) | copy-start | bytes 21508
  88.7 5.9 %collective-permute-start.11 = (f32[2,7,130,1]{2,1,3,0:T(8,128)S(1)}, f32[2,7,130,1]{2,1,3,0:T(8,128)S(1)}, u32[]{:S(2)}, u32[]{:S(2)}) collective-permute-start(f32[2,7,130,1]{2,1,3,0:T(8,128)S(1)} %get-tuple-element.42), channel_id=1, source_target_pairs={{1,0},{2,1},{3,2},{4,3},{5,4},{6,5},{7,6},{9,8},{10,9},{11,10},{12... | collective-permute-start | bytes 21848 | tf_op jit(solution)/shard_map/ppermute | solution.py:23
  127.0 4.9 %collective-permute-start.12 = (f32[2,7,1,128]{3,1,2,0:T(8,128)S(1)}, f32[2,7,1,128]{3,1,2,0:T(8,128)S(1)}, u32[]{:S(2)}, u32[]{:S(2)}) collective-permute-start(f32[2,7,1,128]{3,1,2,0:T(8,128)S(1)} %copy.147), channel_id=1, source_target_pairs={{0,8},{8,16},{16,24},{1,9},{9,17},{17,25},{2,10},{10,18},{18,26},{... | collective-permute-start | bytes 21512 | tf_op jit(solution)/shard_map/ppermute | solution.py:22
  130.6 4.6 %collective-permute-start.13 = (f32[2,7,1,128]{3,1,2,0:T(8,128)S(1)}, f32[2,7,1,128]{3,1,2,0:T(8,128)S(1)}, u32[]{:S(2)}, u32[]{:S(2)}) collective-permute-start(f32[2,7,1,128]{3,1,2,0:T(8,128)S(1)} %copy.149), channel_id=1, source_target_pairs={{8,0},{16,8},{24,16},{9,1},{17,9},{25,17},{10,2},{18,10},{26,18},{... | collective-permute-start | bytes 21512 | tf_op jit(solution)/shard_map/ppermute | solution.py:23
  136.5 5.0 %copy-start.6 = (f32[6,128,128]{1,0,2:T(8,128)S(1)}, f32[6,128,128]{1,0,2:T(8,128)}, u32[]{:S(2)}) copy-start(f32[6,128,128]{1,0,2:T(8,128)} %copy-done.4) | copy-start | bytes 1179652
  136.5 9.2 %copy-start.27 = (f32[2,7,1,128]{2,1,3,0:T(8,128)S(1)}, f32[2,7,1,128]{2,1,3,0:T(8,128)}, u32[]{:S(2)}) copy-start(f32[2,7,1,128]{2,1,3,0:T(8,128)} %copy.148) | copy-start | bytes 21508
  136.5 9.2 %copy-start.28 = (f32[2,7,1,128]{2,1,3,0:T(8,128)S(1)}, f32[2,7,1,128]{2,1,3,0:T(8,128)}, u32[]{:S(2)}) copy-start(f32[2,7,1,128]{2,1,3,0:T(8,128)} %copy.150) | copy-start | bytes 21508
  137.5 4.2 %collective-permute-start.14 = (f32[2,7,130,1]{2,1,3,0:T(8,128)S(1)}, f32[2,7,130,1]{2,1,3,0:T(8,128)S(1)}, u32[]{:S(2)}, u32[]{:S(2)}) collective-permute-start(f32[2,7,130,1]{2,1,3,0:T(8,128)S(1)} %get-tuple-element.39), channel_id=1, source_target_pairs={{0,1},{1,2},{2,3},{3,4},{4,5},{5,6},{6,7},{8,9},{9,10},{10,11},{11... | collective-permute-start | bytes 21848 | tf_op jit(solution)/shard_map/ppermute | solution.py:22
  139.7 6.0 %copy-start.3 = (f32[2,7,128,128]{2,1,3,0:T(8,128)S(1)}, f32[2,7,128,128]{2,1,3,0:T(8,128)}, u32[]{:S(2)}) copy-start(f32[2,7,128,128]{2,1,3,0:T(8,128)} %get-tuple-element.29) | copy-start | bytes 2752516
  139.7 6.0 %copy-start.8 = (f32[7,128,128]{1,0,2:T(8,128)S(1)}, f32[7,128,128]{1,0,2:T(8,128)}, u32[]{:S(2)}) copy-start(f32[7,128,128]{1,0,2:T(8,128)} %copy.119) | copy-start | bytes 1376260
  139.7 6.0 %copy-start.11 = (f32[7,128,128]{1,0,2:T(8,128)S(1)}, f32[7,128,128]{1,0,2:T(8,128)}, u32[]{:S(2)}) copy-start(f32[7,128,128]{1,0,2:T(8,128)} %copy.124) | copy-start | bytes 1376260
  139.7 6.0 %copy-start.14 = (f32[7,128,128]{1,0,2:T(8,128)S(1)}, f32[7,128,128]{1,0,2:T(8,128)}, u32[]{:S(2)}) copy-start(f32[7,128,128]{1,0,2:T(8,128)} %copy.129) | copy-start | bytes 1376260
  139.7 6.0 %copy-start.17 = (f32[7,128,128]{1,0,2:T(8,128)S(1)}, f32[7,128,128]{1,0,2:T(8,128)}, u32[]{:S(2)}) copy-start(f32[7,128,128]{1,0,2:T(8,128)} %copy.134) | copy-start | bytes 1376260
  139.8 6.0 %copy-start.20 = (f32[7,128,128]{1,0,2:T(8,128)S(1)}, f32[7,128,128]{1,0,2:T(8,128)}, u32[]{:S(2)}) copy-start(f32[7,128,128]{1,0,2:T(8,128)} %copy.117) | copy-start | bytes 1376260
  139.8 5.9 %collective-permute-start.15 = (f32[2,7,130,1]{2,1,3,0:T(8,128)S(1)}, f32[2,7,130,1]{2,1,3,0:T(8,128)S(1)}, u32[]{:S(2)}, u32[]{:S(2)}) collective-permute-start(f32[2,7,130,1]{2,1,3,0:T(8,128)S(1)} %get-tuple-element.40), channel_id=1, source_target_pairs={{1,0},{2,1},{3,2},{4,3},{5,4},{6,5},{7,6},{9,8},{10,9},{11,10},{12... | collective-permute-start | bytes 21848 | tf_op jit(solution)/shard_map/ppermute | solution.py:23
  181.0 7.9 %collective-permute-start.17 = (f32[2,7,1,128]{3,1,2,0:T(8,128)S(1)}, f32[2,7,1,128]{3,1,2,0:T(8,128)S(1)}, u32[]{:S(2)}, u32[]{:S(2)}) collective-permute-start(f32[2,7,1,128]{3,1,2,0:T(8,128)S(1)} %copy.155), channel_id=1, source_target_pairs={{8,0},{16,8},{24,16},{9,1},{17,9},{25,17},{10,2},{18,10},{26,18},{... | collective-permute-start | bytes 21512 | tf_op jit(solution)/shard_map/ppermute | solution.py:23
  182.3 5.2 %collective-permute-start.16 = (f32[2,7,1,128]{3,1,2,0:T(8,128)S(1)}, f32[2,7,1,128]{3,1,2,0:T(8,128)S(1)}, u32[]{:S(2)}, u32[]{:S(2)}) collective-permute-start(f32[2,7,1,128]{3,1,2,0:T(8,128)S(1)} %copy.153), channel_id=1, source_target_pairs={{0,8},{8,16},{16,24},{1,9},{9,17},{17,25},{2,10},{10,18},{18,26},{... | collective-permute-start | bytes 21512 | tf_op jit(solution)/shard_map/ppermute | solution.py:22
  190.3 5.3 %copy-start.2 = (f32[7,128,128]{1,0,2:T(8,128)S(1)}, f32[7,128,128]{1,0,2:T(8,128)}, u32[]{:S(2)}) copy-start(f32[7,128,128]{1,0,2:T(8,128)} %copy.139) | copy-start | bytes 1376260
  190.3 5.3 %copy-start.24 = (f32[2,7,128,128]{2,1,3,0:T(8,128)S(1)}, f32[2,7,128,128]{2,1,3,0:T(8,128)}, u32[]{:S(2)}) copy-start(f32[2,7,128,128]{2,1,3,0:T(8,128)} %get-tuple-element.24) | copy-start | bytes 2752516
  190.3 9.6 %copy-start.18 = (f32[7,128,128]{1,0,2:T(8,128)S(1)}, f32[7,128,128]{1,0,2:T(8,128)}, u32[]{:S(2)}) copy-start(f32[7,128,128]{1,0,2:T(8,128)} %copy.134) | copy-start | bytes 1376260
  190.3 9.6 %copy-start.21 = (f32[7,128,128]{1,0,2:T(8,128)S(1)}, f32[7,128,128]{1,0,2:T(8,128)}, u32[]{:S(2)}) copy-start(f32[7,128,128]{1,0,2:T(8,128)} %copy.117) | copy-start | bytes 1376260
  191.3 4.6 %collective-permute-start.18 = (f32[2,7,130,1]{2,1,3,0:T(8,128)S(1)}, f32[2,7,130,1]{2,1,3,0:T(8,128)S(1)}, u32[]{:S(2)}, u32[]{:S(2)}) collective-permute-start(f32[2,7,130,1]{2,1,3,0:T(8,128)S(1)} %get-tuple-element.37), channel_id=1, source_target_pairs={{0,1},{1,2},{2,3},{3,4},{4,5},{5,6},{6,7},{8,9},{9,10},{10,11},{11... | collective-permute-start | bytes 21848 | tf_op jit(solution)/shard_map/ppermute | solution.py:22
  194.3 5.6 %collective-permute-start.19 = (f32[2,7,130,1]{2,1,3,0:T(8,128)S(1)}, f32[2,7,130,1]{2,1,3,0:T(8,128)S(1)}, u32[]{:S(2)}, u32[]{:S(2)}) collective-permute-start(f32[2,7,130,1]{2,1,3,0:T(8,128)S(1)} %get-tuple-element.38), channel_id=1, source_target_pairs={{1,0},{2,1},{3,2},{4,3},{5,4},{6,5},{7,6},{9,8},{10,9},{11,10},{12... | collective-permute-start | bytes 21848 | tf_op jit(solution)/shard_map/ppermute | solution.py:23
  195.6 4.3 %copy-start.9 = (f32[7,128,128]{1,0,2:T(8,128)S(1)}, f32[7,128,128]{1,0,2:T(8,128)}, u32[]{:S(2)}) copy-start(f32[7,128,128]{1,0,2:T(8,128)} %copy.119) | copy-start | bytes 1376260
  195.6 4.3 %copy-start.12 = (f32[7,128,128]{1,0,2:T(8,128)S(1)}, f32[7,128,128]{1,0,2:T(8,128)}, u32[]{:S(2)}) copy-start(f32[7,128,128]{1,0,2:T(8,128)} %copy.124) | copy-start | bytes 1376260
  195.6 4.3 %copy-start.15 = (f32[7,128,128]{1,0,2:T(8,128)S(1)}, f32[7,128,128]{1,0,2:T(8,128)}, u32[]{:S(2)}) copy-start(f32[7,128,128]{1,0,2:T(8,128)} %copy.129) | copy-start | bytes 1376260
  (1 other events, 0.6 us)
